TPU v7x, 32 devices: a whole 2x2x4 slice. The times are simulated.
32 devices in a mesh: row: 8 (over z, x), col: 4 (over y, core).
Axes of the slice: x: 2, y: 2, z: 4, core: 2. Of those that a mesh axis runs over, the one named last changes fastest.
Arguments:
- field: bfloat16 [192, 128, 256], P('row', 'col'), may hold values from -6 to 6
- gains: float32 [1, 2, 256], replicated, may hold values from 0.5 to 1.5
- w_query: bfloat16 [1, 256, 256], replicated, may hold values from -24 to 24
- w_key: bfloat16 [1, 256, 256], replicated, may hold values from -1 to 1
- w_value: bfloat16 [1, 256, 256], replicated, may hold values from -0.375 to 0.375
- w_out: bfloat16 [1, 256, 256], replicated, may hold values from -0.375 to 0.375
- w_up: bfloat16 [1, 256, 1024], replicated, may hold values from -0.375 to 0.375
- w_down: bfloat16 [1, 1024, 256], replicated, may hold values from -0.1875 to 0.1875
- final_gain: float32 [256], replicated, may hold values from 0.5 to 1.5
- conv_weight: bfloat16 [3, 3, 256, 256], replicated, may hold values from -0.125 to 0.125
Outputs:
- image: float32 [16, 768, 512], P(None, 'row', 'col')
All inputs are finite; a program needn't handle non-finite values.
Results may differ from a plain program's by a relative error of at most 0.0056.
Values may be sent and summed in bfloat16 or wider, within the bound.
A program may use at most 64 MiB of HBM per device.

v0:
```python
import jax
import jax.numpy as jnp
from jax import lax
from jax.sharding import PartitionSpec as P

D = 256
HEADS = 8
HEAD = 32
WH = 24
HALO = 8
OUT_CH = 16
SHUF = 4


def extended(block, sides, width):
    for axis, dim in sides:
        count = lax.axis_size(axis)
        forward = [(i, i + 1) for i in range(count - 1)]
        backward = [(target, source) for source, target in forward]
        low = lax.ppermute(
            lax.slice_in_dim(block, block.shape[dim] - width, None, axis=dim), axis, forward
        )
        high = lax.ppermute(lax.slice_in_dim(block, 0, width, axis=dim), axis, backward)
        block = jnp.concatenate([low, block, high], axis=dim)
    return block


def rms(values, gain):
    return values * lax.rsqrt(jnp.mean(values * values, axis=-1, keepdims=True) + 1e-06) * gain


def attend(query, keys, values, valid):
    count = query.shape[0]
    width = keys.shape[0]
    q_heads = query.reshape(count, HEADS, HEAD).transpose(1, 0, 2)
    k_heads = keys.reshape(width, HEADS, HEAD).transpose(1, 0, 2)
    v_heads = values.reshape(width, HEADS, HEAD).transpose(1, 0, 2)

    def one_head(items):
        q_one, k_one, v_one = items
        scores = jnp.dot(q_one, k_one.T, preferred_element_type=jnp.float32) * HEAD ** (-0.5)
        scores = jnp.where(valid[None, :], scores, jnp.float32(-1e30))
        top = jnp.max(scores, axis=-1, keepdims=True)
        expo = jnp.exp(scores - top)
        weights = (expo / jnp.sum(expo, axis=-1, keepdims=True)).astype(jnp.bfloat16)
        return jnp.dot(weights, v_one, preferred_element_type=jnp.float32)

    merged = lax.map(one_head, (q_heads, k_heads, v_heads))
    return merged.transpose(1, 0, 2).reshape(count, HEADS * HEAD).astype(jnp.bfloat16)


def project(flat, weight, tile_rows, tile_cols):
    return (
        jnp.dot(flat, weight, preferred_element_type=jnp.float32)
        .astype(jnp.bfloat16)
        .reshape(tile_rows, tile_cols, D)
    )


def local(field, gains, w_query, w_key, w_value, w_out, w_up, w_down, final_gain, conv_weight):
    tile_rows = field.shape[0]
    tile_cols = field.shape[1]
    rows_all = tile_rows * lax.axis_size("row")
    cols_all = tile_cols * lax.axis_size("col")
    row_pos = (
        lax.axis_index("row") * tile_rows - HALO + jnp.arange(tile_rows + 2 * HALO, dtype=jnp.int32)
    )
    col_pos = (
        lax.axis_index("col") * tile_cols - HALO + jnp.arange(tile_cols + 2 * HALO, dtype=jnp.int32)
    )
    valid = ((row_pos >= 0) & (row_pos < rows_all))[:, None] & (
        (col_pos >= 0) & (col_pos < cols_all)
    )[None, :]
    x = field.astype(jnp.float32)
    normed = rms(x, gains[0, 0]).astype(jnp.bfloat16)
    flat = normed.reshape(-1, D)
    query = project(flat, w_query[0], tile_rows, tile_cols)
    wide = extended(normed, (("row", 0), ("col", 1)), HALO)
    wide_flat = wide.reshape(-1, D)
    keys = project(wide_flat, w_key[0], tile_rows + 2 * HALO, tile_cols + 2 * HALO)
    values = project(wide_flat, w_value[0], tile_rows + 2 * HALO, tile_cols + 2 * HALO)

    def window(index):
        q_block = query.reshape(-1, D)
        k_block = keys.reshape(-1, D)
        v_block = values.reshape(-1, D)
        m_block = valid.reshape(-1)
        return attend(q_block, k_block, v_block, m_block)

    context = lax.map(window, jnp.arange(tile_rows // WH, dtype=jnp.int32)).reshape(-1, D)
    x = x + jnp.dot(context, w_out[0], preferred_element_type=jnp.float32).reshape(
        tile_rows, tile_cols, D
    )
    second_norm = rms(x, gains[0, 1]).astype(jnp.bfloat16).reshape(-1, D)
    hidden = jax.nn.gelu(jnp.dot(second_norm, w_up[0], preferred_element_type=jnp.float32)).astype(
        jnp.bfloat16
    )
    x = x + jnp.dot(hidden, w_down[0], preferred_element_type=jnp.float32).reshape(
        tile_rows, tile_cols, D
    )
    final = rms(x, final_gain).astype(jnp.bfloat16)
    padded = extended(final, (("row", 0), ("col", 1)), 1)
    conv = jnp.zeros((tile_rows * tile_cols, conv_weight.shape[3]), jnp.float32)
    for first in range(3):
        for second in range(3):
            piece = padded[first : first + tile_rows, second : second + tile_cols].reshape(-1, D)
            conv = conv + jnp.dot(
                piece, conv_weight[first, second], preferred_element_type=jnp.float32
            )
    image = conv.reshape(tile_rows, tile_cols, OUT_CH, SHUF, SHUF).transpose(2, 0, 3, 1, 4)
    return image.reshape(OUT_CH, tile_rows * SHUF, tile_cols * SHUF)


def solution(mesh):
    return jax.shard_map(
        local,
        mesh=mesh,
        in_specs=(P("row", "col", None), P(), P(), P(), P(), P(), P(), P(), P(), P()),
        out_specs=P(None, "row", "col"),
        check_vma=False,
    )
```

profile of v0, /device:TPU:1, one launch (start us, length us, event | category | flops | bytes accessed | tf_op | source)
XLA Modules:
  0.0 129.6 jit_solution(2099461376630424536)
XLA Ops:
  3.2 3.9 %collective-permute-start = (bf16[8,32,256]{2,1,0:T(8,128)(2,1)S(1)}, bf16[8,32,256]{2,1,0:T(8,128)(2,1)S(1)}, u32[]{:S(2)}, u32[]{:S(2)}) collective-permute-start(bf16[8,32,256]{2,1,0:T(8,128)(2,1)S(1)} %get-tuple-element.106), channel_id=1, source_target_pairs={{0,4},{4,8},{8,12},{12,16},{16,20},{20,24},{24,28},{1,5},{5,9},{9,... | collective-permute-start | bytes 393224 | tf_op jit(solution)/shard_map/ppermute | solution.py:20
  9.7 3.2 %collective-permute-done.1 = bf16[8,32,256]{2,1,0:T(8,128)(2,1)S(1)} collective-permute-done((bf16[8,32,256]{2,1,0:T(8,128)(2,1)S(1)}, bf16[8,32,256]{2,1,0:T(8,128)(2,1)S(1)}, u32[]{:S(2)}, u32[]{:S(2)}) %collective-permute-start.1) | collective-permute-done | bytes 131104 | tf_op jit(solution)/shard_map/ppermute | solution.py:23
  13.5 5.1 %collective-permute-start.2 = (bf16[40,8,256]{2,1,0:T(8,128)(2,1)}, bf16[40,8,256]{2,1,0:T(8,128)(2,1)S(1)}, u32[]{:S(2)}, u32[]{:S(2)}) collective-permute-start(bf16[40,8,256]{2,1,0:T(8,128)(2,1)} %get-tuple-element.90), channel_id=1, source_target_pairs={{0,1},{1,2},{2,3},{4,5},{5,6},{6,7},{8,9},{9,10},{10,11},{12,13},{... | collective-permute-start | bytes 491528 | tf_op jit(solution)/shard_map/ppermute | solution.py:20
  22.2 3.2 %collective-permute-done.3 = bf16[40,8,256]{2,1,0:T(8,128)(2,1)} collective-permute-done((bf16[40,8,256]{2,1,0:T(8,128)(2,1)S(1)}, bf16[40,8,256]{2,1,0:T(8,128)(2,1)}, u32[]{:S(2)}, u32[]{:S(2)}) %collective-permute-start.3) | collective-permute-done | bytes 163872 | tf_op jit(solution)/shard_map/ppermute | solution.py:23
  28.1 4.6 %copy.18 = bf16[1920,8,32]{2,0,1:T(8,128)(2,1)} copy(bf16[1920,8,32]{0,2,1:T(8,128)(2,1)} %bitcast.129) | data formatting | bytes 1966080 | tf_op jit(solution)/shard_map/while/body/eval_jaxpr/reshape;while/body/eval_jaxpr/reshape;reshape | solution.py:37
  34.1 4.6 %copy.17 = bf16[1920,8,32]{2,0,1:T(8,128)(2,1)} copy(bf16[1920,8,32]{0,2,1:T(8,128)(2,1)} %bitcast.128) | data formatting | bytes 1966080 | tf_op jit(solution)/shard_map/while/body/eval_jaxpr/reshape;while/body/eval_jaxpr/reshape;reshape | solution.py:36
  38.7 50.2 %while.18 = (s32[]{:T(128)}, bf16[8,768,32]{1,2,0:T(8,128)(2,1)S(1)}, bf16[8,768,32]{2,1,0:T(8,128)(2,1)S(1)}, bf16[8,1920,32]{2,1,0:T(8,128)(2,1)}, bf16[8,1920...) while((s32[]{:T(128)}, ...), condition=%wide.region_4.5_spmd.clone, body=%wide.region_1.4_spmd.clone.sunk | while | flops 206438784 | bytes 19004076 | solution.py:48
  38.9 2.3 %fusion.85 = (f32[768]{0:T(1024)S(1)}, f32[768,1920]{1,0:T(8,128)S(1)}) fusion(pred[1920]{0:T(1024)(128)(4,1)S(1)} %broadcast_in_dim.63, bf16[8,1920,32]{2,1,0:T(8,128)(2,1)} %get-tuple-element.183, s32[]{:T(128)} %get-tuple-element.172, bf16[8,768,32]{2,1,0:T(8,128)(2,1)S(1)} %get-tuple-element.182), kind=kOutput, calls=%fused_computation.4.clone.1 | convolution fusion | flops 98794752 | bytes 6592512 | tf_op jit(solution)/shard_map/while/body/eval_jaxpr/while/body/eval_jaxpr/dot_general | solution.py:41
  42.4 2.5 %fusion.87 = bf16[8,768,32]{1,2,0:T(8,128)(2,1)S(1)} fusion(bf16[8,768,32]{1,2,0:T(8,128)(2,1)S(1)} %get-tuple-element.173, s32[]{:T(128)} %get-tuple-element.172, f32[768,1920]{1,0:T(8,128)S(1)} %get-tuple-element.162, f32[768]{0:T(1024)S(1)} %fusion.86, f32[768]{0:T(1024)S(1)} %get-tuple-element.163, pred[1920]{0:T(1024)(128)(4,1)S(1)} %broadcast_in_dim.63, ...), kind=kOutput, calls=%fused_computation.8.clone.1 | convolution fusion | flops 101744640 | bytes 6499328 | tf_op jit(solution)/shard_map/while/body/eval_jaxpr/while/body/eval_jaxpr/dot_general | solution.py:46
  45.2 2.3 %fusion.85 = (f32[768]{0:T(1024)S(1)}, f32[768,1920]{1,0:T(8,128)S(1)}) fusion(pred[1920]{0:T(1024)(128)(4,1)S(1)} %broadcast_in_dim.63, bf16[8,1920,32]{2,1,0:T(8,128)(2,1)} %get-tuple-element.183, s32[]{:T(128)} %get-tuple-element.172, bf16[8,768,32]{2,1,0:T(8,128)(2,1)S(1)} %get-tuple-element.182), kind=kOutput, calls=%fused_computation.4.clone.1 | convolution fusion | flops 98794752 | bytes 6592512 | tf_op jit(solution)/shard_map/while/body/eval_jaxpr/while/body/eval_jaxpr/dot_general | solution.py:41
  48.7 2.5 %fusion.87 = bf16[8,768,32]{1,2,0:T(8,128)(2,1)S(1)} fusion(bf16[8,768,32]{1,2,0:T(8,128)(2,1)S(1)} %get-tuple-element.173, s32[]{:T(128)} %get-tuple-element.172, f32[768,1920]{1,0:T(8,128)S(1)} %get-tuple-element.162, f32[768]{0:T(1024)S(1)} %fusion.86, f32[768]{0:T(1024)S(1)} %get-tuple-element.163, pred[1920]{0:T(1024)(128)(4,1)S(1)} %broadcast_in_dim.63, ...), kind=kOutput, calls=%fused_computation.8.clone.1 | convolution fusion | flops 101744640 | bytes 6499328 | tf_op jit(solution)/shard_map/while/body/eval_jaxpr/while/body/eval_jaxpr/dot_general | solution.py:46
  51.4 2.3 %fusion.85 = (f32[768]{0:T(1024)S(1)}, f32[768,1920]{1,0:T(8,128)S(1)}) fusion(pred[1920]{0:T(1024)(128)(4,1)S(1)} %broadcast_in_dim.63, bf16[8,1920,32]{2,1,0:T(8,128)(2,1)} %get-tuple-element.183, s32[]{:T(128)} %get-tuple-element.172, bf16[8,768,32]{2,1,0:T(8,128)(2,1)S(1)} %get-tuple-element.182), kind=kOutput, calls=%fused_computation.4.clone.1 | convolution fusion | flops 98794752 | bytes 6592512 | tf_op jit(solution)/shard_map/while/body/eval_jaxpr/while/body/eval_jaxpr/dot_general | solution.py:41
  55.0 2.5 %fusion.87 = bf16[8,768,32]{1,2,0:T(8,128)(2,1)S(1)} fusion(bf16[8,768,32]{1,2,0:T(8,128)(2,1)S(1)} %get-tuple-element.173, s32[]{:T(128)} %get-tuple-element.172, f32[768,1920]{1,0:T(8,128)S(1)} %get-tuple-element.162, f32[768]{0:T(1024)S(1)} %fusion.86, f32[768]{0:T(1024)S(1)} %get-tuple-element.163, pred[1920]{0:T(1024)(128)(4,1)S(1)} %broadcast_in_dim.63, ...), kind=kOutput, calls=%fused_computation.8.clone.1 | convolution fusion | flops 101744640 | bytes 6499328 | tf_op jit(solution)/shard_map/while/body/eval_jaxpr/while/body/eval_jaxpr/dot_general | solution.py:46
  57.7 2.3 %fusion.85 = (f32[768]{0:T(1024)S(1)}, f32[768,1920]{1,0:T(8,128)S(1)}) fusion(pred[1920]{0:T(1024)(128)(4,1)S(1)} %broadcast_in_dim.63, bf16[8,1920,32]{2,1,0:T(8,128)(2,1)} %get-tuple-element.183, s32[]{:T(128)} %get-tuple-element.172, bf16[8,768,32]{2,1,0:T(8,128)(2,1)S(1)} %get-tuple-element.182), kind=kOutput, calls=%fused_computation.4.clone.1 | convolution fusion | flops 98794752 | bytes 6592512 | tf_op jit(solution)/shard_map/while/body/eval_jaxpr/while/body/eval_jaxpr/dot_general | solution.py:41
  61.3 2.5 %fusion.87 = bf16[8,768,32]{1,2,0:T(8,128)(2,1)S(1)} fusion(bf16[8,768,32]{1,2,0:T(8,128)(2,1)S(1)} %get-tuple-element.173, s32[]{:T(128)} %get-tuple-element.172, f32[768,1920]{1,0:T(8,128)S(1)} %get-tuple-element.162, f32[768]{0:T(1024)S(1)} %fusion.86, f32[768]{0:T(1024)S(1)} %get-tuple-element.163, pred[1920]{0:T(1024)(128)(4,1)S(1)} %broadcast_in_dim.63, ...), kind=kOutput, calls=%fused_computation.8.clone.1 | convolution fusion | flops 101744640 | bytes 6499328 | tf_op jit(solution)/shard_map/while/body/eval_jaxpr/while/body/eval_jaxpr/dot_general | solution.py:46
  64.0 2.3 %fusion.85 = (f32[768]{0:T(1024)S(1)}, f32[768,1920]{1,0:T(8,128)S(1)}) fusion(pred[1920]{0:T(1024)(128)(4,1)S(1)} %broadcast_in_dim.63, bf16[8,1920,32]{2,1,0:T(8,128)(2,1)} %get-tuple-element.183, s32[]{:T(128)} %get-tuple-element.172, bf16[8,768,32]{2,1,0:T(8,128)(2,1)S(1)} %get-tuple-element.182), kind=kOutput, calls=%fused_computation.4.clone.1 | convolution fusion | flops 98794752 | bytes 6592512 | tf_op jit(solution)/shard_map/while/body/eval_jaxpr/while/body/eval_jaxpr/dot_general | solution.py:41
  67.6 2.5 %fusion.87 = bf16[8,768,32]{1,2,0:T(8,128)(2,1)S(1)} fusion(bf16[8,768,32]{1,2,0:T(8,128)(2,1)S(1)} %get-tuple-element.173, s32[]{:T(128)} %get-tuple-element.172, f32[768,1920]{1,0:T(8,128)S(1)} %get-tuple-element.162, f32[768]{0:T(1024)S(1)} %fusion.86, f32[768]{0:T(1024)S(1)} %get-tuple-element.163, pred[1920]{0:T(1024)(128)(4,1)S(1)} %broadcast_in_dim.63, ...), kind=kOutput, calls=%fused_computation.8.clone.1 | convolution fusion | flops 101744640 | bytes 6499328 | tf_op jit(solution)/shard_map/while/body/eval_jaxpr/while/body/eval_jaxpr/dot_general | solution.py:46
  70.3 2.3 %fusion.85 = (f32[768]{0:T(1024)S(1)}, f32[768,1920]{1,0:T(8,128)S(1)}) fusion(pred[1920]{0:T(1024)(128)(4,1)S(1)} %broadcast_in_dim.63, bf16[8,1920,32]{2,1,0:T(8,128)(2,1)} %get-tuple-element.183, s32[]{:T(128)} %get-tuple-element.172, bf16[8,768,32]{2,1,0:T(8,128)(2,1)S(1)} %get-tuple-element.182), kind=kOutput, calls=%fused_computation.4.clone.1 | convolution fusion | flops 98794752 | bytes 6592512 | tf_op jit(solution)/shard_map/while/body/eval_jaxpr/while/body/eval_jaxpr/dot_general | solution.py:41
  73.8 2.5 %fusion.87 = bf16[8,768,32]{1,2,0:T(8,128)(2,1)S(1)} fusion(bf16[8,768,32]{1,2,0:T(8,128)(2,1)S(1)} %get-tuple-element.173, s32[]{:T(128)} %get-tuple-element.172, f32[768,1920]{1,0:T(8,128)S(1)} %get-tuple-element.162, f32[768]{0:T(1024)S(1)} %fusion.86, f32[768]{0:T(1024)S(1)} %get-tuple-element.163, pred[1920]{0:T(1024)(128)(4,1)S(1)} %broadcast_in_dim.63, ...), kind=kOutput, calls=%fused_computation.8.clone.1 | convolution fusion | flops 101744640 | bytes 6499328 | tf_op jit(solution)/shard_map/while/body/eval_jaxpr/while/body/eval_jaxpr/dot_general | solution.py:46
  76.6 2.3 %fusion.85 = (f32[768]{0:T(1024)S(1)}, f32[768,1920]{1,0:T(8,128)S(1)}) fusion(pred[1920]{0:T(1024)(128)(4,1)S(1)} %broadcast_in_dim.63, bf16[8,1920,32]{2,1,0:T(8,128)(2,1)} %get-tuple-element.183, s32[]{:T(128)} %get-tuple-element.172, bf16[8,768,32]{2,1,0:T(8,128)(2,1)S(1)} %get-tuple-element.182), kind=kOutput, calls=%fused_computation.4.clone.1 | convolution fusion | flops 98794752 | bytes 6592512 | tf_op jit(solution)/shard_map/while/body/eval_jaxpr/while/body/eval_jaxpr/dot_general | solution.py:41
  80.1 2.5 %fusion.87 = bf16[8,768,32]{1,2,0:T(8,128)(2,1)S(1)} fusion(bf16[8,768,32]{1,2,0:T(8,128)(2,1)S(1)} %get-tuple-element.173, s32[]{:T(128)} %get-tuple-element.172, f32[768,1920]{1,0:T(8,128)S(1)} %get-tuple-element.162, f32[768]{0:T(1024)S(1)} %fusion.86, f32[768]{0:T(1024)S(1)} %get-tuple-element.163, pred[1920]{0:T(1024)(128)(4,1)S(1)} %broadcast_in_dim.63, ...), kind=kOutput, calls=%fused_computation.8.clone.1 | convolution fusion | flops 101744640 | bytes 6499328 | tf_op jit(solution)/shard_map/while/body/eval_jaxpr/while/body/eval_jaxpr/dot_general | solution.py:46
  82.8 2.3 %fusion.85 = (f32[768]{0:T(1024)S(1)}, f32[768,1920]{1,0:T(8,128)S(1)}) fusion(pred[1920]{0:T(1024)(128)(4,1)S(1)} %broadcast_in_dim.63, bf16[8,1920,32]{2,1,0:T(8,128)(2,1)} %get-tuple-element.183, s32[]{:T(128)} %get-tuple-element.172, bf16[8,768,32]{2,1,0:T(8,128)(2,1)S(1)} %get-tuple-element.182), kind=kOutput, calls=%fused_computation.4.clone.1 | convolution fusion | flops 98794752 | bytes 6592512 | tf_op jit(solution)/shard_map/while/body/eval_jaxpr/while/body/eval_jaxpr/dot_general | solution.py:41
  86.4 2.5 %fusion.87 = bf16[8,768,32]{1,2,0:T(8,128)(2,1)S(1)} fusion(bf16[8,768,32]{1,2,0:T(8,128)(2,1)S(1)} %get-tuple-element.173, s32[]{:T(128)} %get-tuple-element.172, f32[768,1920]{1,0:T(8,128)S(1)} %get-tuple-element.162, f32[768]{0:T(1024)S(1)} %fusion.86, f32[768]{0:T(1024)S(1)} %get-tuple-element.163, pred[1920]{0:T(1024)(128)(4,1)S(1)} %broadcast_in_dim.63, ...), kind=kOutput, calls=%fused_computation.8.clone.1 | convolution fusion | flops 101744640 | bytes 6499328 | tf_op jit(solution)/shard_map/while/body/eval_jaxpr/while/body/eval_jaxpr/dot_general | solution.py:46
  89.7 2.2 %reshape.112 = bf16[24,32,256]{1,0,2:T(8,128)(2,1)S(1)} reshape(bf16[768,8,32]{0,2,1:T(8,128)(2,1)} %bitcast.142) | data formatting | bytes 786432 | tf_op jit(solution)/shard_map/while/body/eval_jaxpr/convert_element_type | solution.py:49
  94.9 4.2 %collective-permute-start.4 = (bf16[1,32,256]{2,1,0:T(8,128)(2,1)S(1)}, bf16[1,32,256]{2,1,0:T(8,128)(2,1)S(1)}, u32[]{:S(2)}, u32[]{:S(2)}) collective-permute-start(bf16[1,32,256]{2,1,0:T(8,128)(2,1)S(1)} %get-tuple-element.104), channel_id=1, source_target_pairs={{0,4},{4,8},{8,12},{12,16},{16,20},{20,24},{24,28},{1,5},{5,9},{9,... | collective-permute-start | bytes 49160 | tf_op jit(solution)/shard_map/ppermute | solution.py:20
  100.4 3.2 %collective-permute-done.5 = bf16[1,32,256]{2,1,0:T(8,128)(2,1)S(1)} collective-permute-done((bf16[1,32,256]{2,1,0:T(8,128)(2,1)S(1)}, bf16[1,32,256]{2,1,0:T(8,128)(2,1)S(1)}, u32[]{:S(2)}, u32[]{:S(2)}) %collective-permute-start.5) | collective-permute-done | bytes 16416 | tf_op jit(solution)/shard_map/ppermute | solution.py:23
  103.6 3.1 %collective-permute-start.6 = (bf16[26,1,256]{2,1,0:T(2,128)(2,1)S(1)}, bf16[26,1,256]{2,1,0:T(2,128)(2,1)S(1)}, u32[]{:S(2)}, u32[]{:S(2)}) collective-permute-start(bf16[26,1,256]{2,1,0:T(2,128)(2,1)S(1)} %get-tuple-element.100), channel_id=1, source_target_pairs={{0,1},{1,2},{2,3},{4,5},{5,6},{6,7},{8,9},{9,10},{10,11},{12,13},{... | collective-permute-start | bytes 39944 | tf_op jit(solution)/shard_map/ppermute | solution.py:20
  106.7 2.1 %collective-permute-start.7 = (bf16[26,1,256]{2,1,0:T(2,128)(2,1)S(1)}, bf16[26,1,256]{2,1,0:T(2,128)(2,1)S(1)}, u32[]{:S(2)}, u32[]{:S(2)}) collective-permute-start(bf16[26,1,256]{2,1,0:T(2,128)(2,1)S(1)} %get-tuple-element.101), channel_id=1, source_target_pairs={{1,0},{2,1},{3,2},{5,4},{6,5},{7,6},{9,8},{10,9},{11,10},{13,12},{... | collective-permute-start | bytes 39944 | tf_op jit(solution)/shard_map/ppermute | solution.py:23
  109.2 2.7 %collective-permute-done.7 = bf16[26,1,256]{2,1,0:T(2,128)(2,1)S(1)} collective-permute-done((bf16[26,1,256]{2,1,0:T(2,128)(2,1)S(1)}, bf16[26,1,256]{2,1,0:T(2,128)(2,1)S(1)}, u32[]{:S(2)}, u32[]{:S(2)}) %collective-permute-start.7) | collective-permute-done | bytes 13344 | tf_op jit(solution)/shard_map/ppermute | solution.py:23
  115.0 2.6 %reshape.108 = f32[24,32,16,4,4]{1,0,4,3,2:T(8,128)} reshape(f32[768,256]{0,1:T(8,128)S(1)} %copy.20) | data formatting | bytes 1572864 | tf_op jit(solution)/shard_map/reshape | solution.py:110
  117.6 6.7 %copy.21 = f32[16,24,4,32,4]{0,4,3,2,1:T(4,128)} copy(f32[16,24,4,32,4]{3,1,4,2,0:T(8,128)} %bitcast.121) | data formatting | bytes 1572864 | tf_op jit(solution)/shard_map/transpose | solution.py:110
  124.3 5.3 %copy.22 = f32[16,96,128]{2,1,0:T(8,128)} copy(f32[16,96,128]{0,2,1:T(8,128)} %bitcast.120) | data formatting | bytes 1572864 | tf_op jit(solution)/shard_map/reshape | solution.py:111
  (93 shorter events, 33.8 us)
Async XLA Ops:
  0.0 92.8 %copy-start = (bf16[1,256,1024]{2,1,0:T(8,128)(2,1)S(1)}, bf16[1,256,1024]{2,1,0:T(8,128)(2,1)}, u32[]{:S(2)}) copy-start(bf16[1,256,1024]{2,1,0:T(8,128)(2,1)} %param.18) | copy-start | bytes 1572868
  3.2 6.5 %collective-permute-start = (bf16[8,32,256]{2,1,0:T(8,128)(2,1)S(1)}, bf16[8,32,256]{2,1,0:T(8,128)(2,1)S(1)}, u32[]{:S(2)}, u32[]{:S(2)}) collective-permute-start(bf16[8,32,256]{2,1,0:T(8,128)(2,1)S(1)} %get-tuple-element.106), channel_id=1, source_target_pairs={{0,4},{4,8},{8,12},{12,16},{16,20},{20,24},{24,28},{1,5},{5,9},{9,... | collective-permute-start | bytes 393224 | tf_op jit(solution)/shard_map/ppermute | solution.py:20
  7.1 5.7 %collective-permute-start.1 = (bf16[8,32,256]{2,1,0:T(8,128)(2,1)S(1)}, bf16[8,32,256]{2,1,0:T(8,128)(2,1)S(1)}, u32[]{:S(2)}, u32[]{:S(2)}) collective-permute-start(bf16[8,32,256]{2,1,0:T(8,128)(2,1)S(1)} %get-tuple-element.107), channel_id=1, source_target_pairs={{4,0},{8,4},{12,8},{16,12},{20,16},{24,20},{28,24},{5,1},{9,5},{13... | collective-permute-start | bytes 393224 | tf_op jit(solution)/shard_map/ppermute | solution.py:23
  9.6 11.9 %copy-start.4 = (bf16[8,32,256]{2,1,0:T(8,128)(2,1)}, bf16[8,32,256]{2,1,0:T(8,128)(2,1)S(1)}, u32[]{:S(2)}) copy-start(bf16[8,32,256]{2,1,0:T(8,128)(2,1)S(1)} %collective-permute-done) | copy-start | bytes 393220
  12.8 8.7 %copy-start.5 = (bf16[8,32,256]{2,1,0:T(8,128)(2,1)}, bf16[8,32,256]{2,1,0:T(8,128)(2,1)S(1)}, u32[]{:S(2)}) copy-start(bf16[8,32,256]{2,1,0:T(8,128)(2,1)S(1)} %collective-permute-done.1) | copy-start | bytes 393220
  13.5 8.0 %collective-permute-start.2 = (bf16[40,8,256]{2,1,0:T(8,128)(2,1)}, bf16[40,8,256]{2,1,0:T(8,128)(2,1)S(1)}, u32[]{:S(2)}, u32[]{:S(2)}) collective-permute-start(bf16[40,8,256]{2,1,0:T(8,128)(2,1)} %get-tuple-element.90), channel_id=1, source_target_pairs={{0,1},{1,2},{2,3},{4,5},{5,6},{6,7},{8,9},{9,10},{10,11},{12,13},{... | collective-permute-start | bytes 491528 | tf_op jit(solution)/shard_map/ppermute | solution.py:20
  18.7 6.7 %collective-permute-start.3 = (bf16[40,8,256]{2,1,0:T(8,128)(2,1)S(1)}, bf16[40,8,256]{2,1,0:T(8,128)(2,1)}, u32[]{:S(2)}, u32[]{:S(2)}) collective-permute-start(bf16[40,8,256]{2,1,0:T(8,128)(2,1)S(1)} %get-tuple-element.91), channel_id=1, source_target_pairs={{1,0},{2,1},{3,2},{5,4},{6,5},{7,6},{9,8},{10,9},{11,10},{13,12},{... | collective-permute-start | bytes 491528 | tf_op jit(solution)/shard_map/ppermute | solution.py:23
  21.5 5.1 %copy-start.9 = (bf16[1,256,256]{2,1,0:T(8,128)(2,1)S(1)}, bf16[1,256,256]{2,1,0:T(8,128)(2,1)}, u32[]{:S(2)}) copy-start(bf16[1,256,256]{2,1,0:T(8,128)(2,1)} %param.16) | copy-start | bytes 393220
  21.5 0.7 copy-start.8
  28.1 4.6 %copy-start.10 = (bf16[1,256,256]{2,1,0:T(8,128)(2,1)S(1)}, bf16[1,256,256]{2,1,0:T(8,128)(2,1)}, u32[]{:S(2)}) copy-start(bf16[1,256,256]{2,1,0:T(8,128)(2,1)} %param.15) | copy-start | bytes 393220
  34.1 4.6 %copy-start.6 = (bf16[8,768,32]{1,2,0:T(8,128)(2,1)S(1)}, bf16[8,768,32]{1,2,0:T(8,128)(2,1)}, u32[]{:S(2)}) copy-start(bf16[8,768,32]{1,2,0:T(8,128)(2,1)} %custom-call) | copy-start | bytes 1179652
  89.0 0.7 copy-start.7
  89.0 2.9 %copy-start.1 = (bf16[24,32,256]{2,1,0:T(8,128)(2,1)S(1)}, bf16[24,32,256]{2,1,0:T(8,128)(2,1)}, u32[]{:S(2)}) copy-start(bf16[24,32,256]{2,1,0:T(8,128)(2,1)} %param.12) | copy-start | bytes 1179652
  89.0 2.9 %copy-start.11 = (bf16[1,256,256]{2,1,0:T(8,128)(2,1)S(1)}, bf16[1,256,256]{2,1,0:T(8,128)(2,1)}, u32[]{:S(2)}) copy-start(bf16[1,256,256]{2,1,0:T(8,128)(2,1)} %param.17) | copy-start | bytes 393220
  92.8 1.2 copy-start.3
  94.0 0.7 copy-start.12
  94.7 14.2 %copy-start.2 = (bf16[3,3,256,256]{3,2,1,0:T(8,128)(2,1)S(1)}, bf16[3,3,256,256]{3,2,1,0:T(8,128)(2,1)}, u32[]{:S(2)}) copy-start(bf16[3,3,256,256]{3,2,1,0:T(8,128)(2,1)} %param.21) | copy-start | bytes 3538948
  94.9 5.5 %collective-permute-start.4 = (bf16[1,32,256]{2,1,0:T(8,128)(2,1)S(1)}, bf16[1,32,256]{2,1,0:T(8,128)(2,1)S(1)}, u32[]{:S(2)}, u32[]{:S(2)}) collective-permute-start(bf16[1,32,256]{2,1,0:T(8,128)(2,1)S(1)} %get-tuple-element.104), channel_id=1, source_target_pairs={{0,4},{4,8},{8,12},{12,16},{16,20},{20,24},{24,28},{1,5},{5,9},{9,... | collective-permute-start | bytes 49160 | tf_op jit(solution)/shard_map/ppermute | solution.py:20
  99.1 4.5 %collective-permute-start.5 = (bf16[1,32,256]{2,1,0:T(8,128)(2,1)S(1)}, bf16[1,32,256]{2,1,0:T(8,128)(2,1)S(1)}, u32[]{:S(2)}, u32[]{:S(2)}) collective-permute-start(bf16[1,32,256]{2,1,0:T(8,128)(2,1)S(1)} %get-tuple-element.105), channel_id=1, source_target_pairs={{4,0},{8,4},{12,8},{16,12},{20,16},{24,20},{28,24},{5,1},{9,5},{13... | collective-permute-start | bytes 49160 | tf_op jit(solution)/shard_map/ppermute | solution.py:23
  103.6 5.5 %collective-permute-start.6 = (bf16[26,1,256]{2,1,0:T(2,128)(2,1)S(1)}, bf16[26,1,256]{2,1,0:T(2,128)(2,1)S(1)}, u32[]{:S(2)}, u32[]{:S(2)}) collective-permute-start(bf16[26,1,256]{2,1,0:T(2,128)(2,1)S(1)} %get-tuple-element.100), channel_id=1, source_target_pairs={{0,1},{1,2},{2,3},{4,5},{5,6},{6,7},{8,9},{9,10},{10,11},{12,13},{... | collective-permute-start | bytes 39944 | tf_op jit(solution)/shard_map/ppermute | solution.py:20
  106.7 5.2 %collective-permute-start.7 = (bf16[26,1,256]{2,1,0:T(2,128)(2,1)S(1)}, bf16[26,1,256]{2,1,0:T(2,128)(2,1)S(1)}, u32[]{:S(2)}, u32[]{:S(2)}) collective-permute-start(bf16[26,1,256]{2,1,0:T(2,128)(2,1)S(1)} %get-tuple-element.101), channel_id=1, source_target_pairs={{1,0},{2,1},{3,2},{5,4},{6,5},{7,6},{9,8},{10,9},{11,10},{13,12},{... | collective-permute-start | bytes 39944 | tf_op jit(solution)/shard_map/ppermute | solution.py:23
where the time goes:
time: 131 us; the launch traced here: 130 us
  matrix products  47.6 us (36%)
  local copies, waits for them, and re-layouts  30.3 us (23%)
  starting transfers between devices  22.9 us (17%)
  other arithmetic  15.9 us (12%)
  waiting for transfers between devices  12.3 us (9%)
    dot_general x8, matrix products, one_head(): return jnp.dot(weights, v_one, preferred_element_type=jnp.float32)  20.3 us
    dot_general x8, matrix products, one_head(): jnp.dot(q_one, k_one.T, preferred_element_type=jnp.float32) * HEAD ** (-0.5)  18.2 us
    ppermute x4, starting transfers between devices, extended(): lax.ppermute(lax.slice_in_dim(block, block.shape[dim] - width, None, axis...  16.3 us
    ppermute x4, waiting for transfers between devices, extended(): lax.ppermute(lax.slice_in_dim(block, 0, width, axis=dim), axis, backward)  12.3 us
    reduce_sum x8, other arithmetic, one_head(): jnp.sum(expo, axis=-1, keepdims=True)  10.3 us
    transpose x1, local copies, waits for them, and re-layouts, local(): conv.reshape(tile_rows, tile_cols, OUT_CH, SHUF, SHUF)  6.74 us
    ppermute x4, starting transfers between devices, extended(): lax.ppermute(lax.slice_in_dim(block, 0, width, axis=dim), axis, backward)  6.61 us
    reshape x1, local copies, waits for them, and re-layouts, local(): return image.reshape(OUT_CH, tile_rows * SHUF, tile_cols * SHUF)  5.31 us
  transfers between devices with their start and end apart: 8, of which 4 were waited for; matrix products, arithmetic and copies ran while one was open for 2% of the time, Pallas kernels for 0%

commit v1 on v0

v1 whole, which is shorter than its diff:
```python
import functools

import jax
import jax.numpy as jnp
from jax import lax
from jax.experimental import pallas as pl
from jax.experimental.pallas import tpu as pltpu
from jax.sharding import PartitionSpec as P

HEADS = 8
HALO = 8
SHUF = 4
CHUNK = 128
VMEM_LIMIT = 56 * 1024 * 1024
BF = jnp.bfloat16
F32 = jnp.float32
NEIGHBOURS = ((-1, 0), (1, 0), (0, -1), (0, 1), (-1, -1), (-1, 1), (1, -1), (1, 1))


def rms(values, gain):
    return values * lax.rsqrt(jnp.mean(values * values, axis=-1, keepdims=True) + 1e-06) * gain


def there(step, sizes):
    row, col = lax.axis_index("row"), lax.axis_index("col")
    nrow, ncol = row + step[0], col + step[1]
    ok = (nrow >= 0) & (nrow < sizes[0]) & (ncol >= 0) & (ncol < sizes[1])
    return ok, nrow, ncol


def greet(sizes):
    barrier = pltpu.get_barrier_semaphore()
    for step in NEIGHBOURS:
        ok, nrow, ncol = there(step, sizes)

        @pl.when(ok)
        def _():
            pl.semaphore_signal(
                barrier, inc=1, device_id=(nrow, ncol), device_id_type=pl.DeviceIdType.MESH
            )

    peers = jnp.int32(0)
    for step in NEIGHBOURS:
        peers = peers + there(step, sizes)[0].astype(jnp.int32)
    pl.semaphore_wait(barrier, peers)


def swap(sizes, sources, slots, send, recv, fills):
    copies = []
    for n, step in enumerate(NEIGHBOURS):
        ok, nrow, ncol = there(step, sizes)
        back = NEIGHBOURS.index((-step[0], -step[1]))
        copy = pltpu.make_async_remote_copy(
            src_ref=sources[n],
            dst_ref=slots[back],
            send_sem=send.at[n],
            recv_sem=recv.at[back],
            device_id=(nrow, ncol),
            device_id_type=pl.DeviceIdType.MESH,
        )
        arrival = pltpu.make_async_remote_copy(
            src_ref=slots[n],
            dst_ref=slots[n],
            send_sem=send.at[n],
            recv_sem=recv.at[n],
            device_id=(nrow, ncol),
            device_id_type=pl.DeviceIdType.MESH,
        )
        copies.append((ok, copy, arrival))
        pl.when(ok)(copy.start)
        pl.when(jnp.logical_not(ok))(fills[n])
    return copies


def finish(copies):
    for ok, copy, arrival in copies:
        pl.when(ok)(arrival.wait_recv)
    for ok, copy, _ in copies:
        pl.when(ok)(copy.wait_send)


def pieces(rows, groups):
    return [HALO * groups] * 2 + [rows] * 2 + [HALO] * 4


def halo_kernel(sizes, field_ref, halo_ref, send, recv):
    rows, groups = field_ref.shape[:2]
    greet(sizes)
    sources, slots, fills = [], [], []
    first = 0
    for step, count in zip(NEIGHBOURS, pieces(rows, groups)):
        dr, dc = step
        rsel = slice(0, rows) if dr == 0 else (slice(0, HALO) if dr < 0 else slice(rows - HALO, rows))
        slot = halo_ref.at[pl.ds(first, count)]
        if dc == 0:
            sources.append(field_ref.at[rsel])
            slot4 = halo_ref.at[pl.ds(first, count)].reshape(HALO, groups, 8, field_ref.shape[3])
            slots.append(slot4)
        else:
            sources.append(field_ref.at[rsel, 0 if dc < 0 else groups - 1])
            slots.append(slot)

        def fill(first=first, count=count):
            for k in range(0, count, HALO):
                halo_ref[first + k : first + k + HALO] = field_ref[0:HALO, 0]

        fills.append(fill)
        first += count
    finish(swap(sizes, sources, slots, send, recv, fills))


def halo_exchange(sizes, field):
    rows, cols, width = field.shape
    groups = cols // 8
    blocks = sum(pieces(rows, groups))
    return pl.pallas_call(
        functools.partial(halo_kernel, sizes),
        out_shape=jax.ShapeDtypeStruct((blocks, 8, width), BF),
        in_specs=[pl.BlockSpec(memory_space=pltpu.VMEM)],
        out_specs=pl.BlockSpec(memory_space=pltpu.VMEM),
        scratch_shapes=[pltpu.SemaphoreType.DMA((8,)), pltpu.SemaphoreType.DMA((8,))],
        compiler_params=pltpu.CompilerParams(collective_id=0, has_side_effects=True),
        name="halo_exchange",
    )(field.reshape(rows, groups, 8, width))


def layer_kernel(
    sizes, rows, cols,
    field_ref, halo_ref, gains_ref, wq_ref, wk_ref, wv_ref, wo_ref, wu_ref, wd_ref, fg_ref,
    out_ref, left_ref, right_ref,
    q_s, kt_s, va_s, f_s,
):
    tokens, width = field_ref.shape
    head = width // HEADS
    per = 128 // head
    g0 = gains_ref[0:1, :]
    g1 = gains_ref[1:2, :]
    fg = fg_ref[...]
    lane = lax.broadcasted_iota(jnp.int32, (1, 128), 1) // head

    def keep(h, start, ok):
        k = jnp.dot(h, wk_ref[...], preferred_element_type=F32)
        kt_s[:, start : start + h.shape[0]] = k.T.astype(BF)
        v = jnp.dot(h, wv_ref[...], preferred_element_type=F32)
        for e in range(HEADS):
            half = e // per
            part = jnp.where(lane == e % per, v[:, half * 128 : half * 128 + 128], 1.0)
            if ok is not None:
                part = part * ok
            va_s[e, start : start + h.shape[0], :] = part.astype(BF)

    scale = head**-0.5 * 1.4426950408889634
    for start in range(0, tokens, 256):
        h = rms(field_ref[start : start + 256, :].astype(F32), g0).astype(BF)
        q = jnp.dot(h, wq_ref[...], preferred_element_type=F32) * scale
        q_s[start : start + 256, :] = q.astype(BF)
        keep(h, start, None)
    first = 0
    groups = cols // 8
    marks = []
    for step, count in zip(NEIGHBOURS, pieces(rows, groups)):
        ok = there(step, sizes)[0].astype(F32)
        marks.append((first * 8, count * 8, ok))
        first += count
    total = first * 8
    for start in range(0, total, 128):
        h = rms(halo_ref[start : start + 128, :].astype(F32), g0).astype(BF)
        row = lax.broadcasted_iota(jnp.int32, (128, 1), 0) + start
        ok = jnp.zeros((128, 1), F32)
        for at, count, flag in marks:
            if at < start + 128 and at + count > start:
                ok = jnp.where((row >= at) & (row < at + count), flag, ok)
        keep(h, tokens + start, ok)

    def body(index, carry):
        at = pl.ds(pl.multiple_of(index * CHUNK, CHUNK), CHUNK)
        halves = []
        for half in range(width // 128):
            qh = q_s[at, half * 128 : half * 128 + 128]
            ctx = jnp.zeros((CHUNK, 128), F32)
            for e in range(per):
                qm = jnp.where(lane == e, qh, jnp.zeros_like(qh))
                s = jnp.dot(qm, kt_s[half * 128 : half * 128 + 128, :], preferred_element_type=F32)
                m = jnp.max(s, axis=-1, keepdims=True)
                p = jnp.exp2(s - m).astype(BF)
                o = jnp.dot(p, va_s[half * per + e], preferred_element_type=F32)
                ctx = jnp.where(lane == e, o / pltpu.roll(o, head, 1), ctx)
            halves.append(ctx.astype(BF))
        ctx = jnp.concatenate(halves, axis=1)
        x = field_ref[at, :].astype(F32) + jnp.dot(ctx, wo_ref[...], preferred_element_type=F32)
        h = rms(x, g1).astype(BF)
        u = jax.nn.gelu(jnp.dot(h, wu_ref[...], preferred_element_type=F32)).astype(BF)
        x = x + jnp.dot(u, wd_ref[...], preferred_element_type=F32)
        f = rms(x, fg)
        out_ref[at, :] = f.astype(BF)
        for half in range(width // 128):
            f_s[half, at, :] = f[:, half * 128 : half * 128 + 128]
        return carry

    lax.fori_loop(0, tokens // CHUNK, body, 0)
    for half in range(width // 128):
        sl = slice(half * 128, half * 128 + 128)
        left_ref[:, sl] = f_s[half, pl.ds(0, rows, stride=cols), :].astype(BF)
        right_ref[:, sl] = f_s[half, pl.ds(cols - 1, rows, stride=cols), :].astype(BF)


def layer(sizes, rows, cols, field, halo, gains, wq, wk, wv, wo, wu, wd, fg):
    tokens, width = field.shape
    keys = tokens + halo.shape[0]
    vm = pl.BlockSpec(memory_space=pltpu.VMEM)
    return pl.pallas_call(
        functools.partial(layer_kernel, sizes, rows, cols),
        out_shape=(
            jax.ShapeDtypeStruct((tokens, width), BF),
            jax.ShapeDtypeStruct((rows, width), BF),
            jax.ShapeDtypeStruct((rows, width), BF),
        ),
        in_specs=[vm] * 10,
        out_specs=(vm, vm, vm),
        scratch_shapes=[
            pltpu.VMEM((tokens, width), BF),
            pltpu.VMEM((width, keys), BF),
            pltpu.VMEM((HEADS, keys, 128), BF),
            pltpu.VMEM((width // 128, tokens, 128), F32),
        ],
        compiler_params=pltpu.CompilerParams(vmem_limit_bytes=VMEM_LIMIT),
        name="layer",
    )(field, halo, gains, wq, wk, wv, wo, wu, wd, fg)


def conv_kernel(
    sizes,
    final_ref, left_ref, right_ref, weight_ref,
    image_ref,
    row_h, col_h, cor_h, fb_s, wp_s, up_s, send, recv,
):
    rows, cols, width = final_ref.shape
    tokens = rows * cols
    outs = weight_ref.shape[1]
    greet(sizes)
    slots = [row_h.at[0], row_h.at[1], col_h.at[0], col_h.at[1]] + [cor_h.at[n] for n in range(4)]
    sources = [
        final_ref.at[0], final_ref.at[rows - 1], left_ref, right_ref,
        left_ref.at[pl.ds(0, 8)], right_ref.at[pl.ds(0, 8)],
        left_ref.at[pl.ds(rows - 8, 8)], right_ref.at[pl.ds(rows - 8, 8)],
    ]

    def filler(slot):
        def fill():
            slot[...] = jnp.zeros(slot.shape, BF)
        return fill

    copies = swap(sizes, sources, slots, send, recv, [filler(s) for s in slots])
    old = lax.broadcasted_iota(jnp.int32, (outs, outs), 0)
    new = lax.broadcasted_iota(jnp.int32, (outs, outs), 1)
    want = (new % (outs // SHUF)) * SHUF + new // (outs // SHUF)
    perm = jnp.where(old == want, 1.0, 0.0).astype(BF)
    for tap in range(9):
        sl = slice(tap * width, (tap + 1) * width)
        wp_s[sl, :] = jnp.dot(weight_ref[sl, :], perm, preferred_element_type=F32).astype(BF)
    finish(copies)

    col = lax.broadcasted_iota(jnp.int32, (1, cols, 1), 1)

    def spread(first, count, x, before, after):
        flat = x.reshape(count * cols, width)
        low = pltpu.roll(flat, 1, 0).reshape(count, cols, width)
        high = pltpu.roll(flat, count * cols - 1, 0).reshape(count, cols, width)
        fb_s[1, first : first + count] = x.astype(BF)
        fb_s[0, first : first + count] = jnp.where(col == 0, before, low).astype(BF)
        fb_s[2, first : first + count] = jnp.where(col == cols - 1, after, high).astype(BF)

    for r in range(0, rows, 8):
        before = col_h[0, r : r + 8, :].astype(F32)[:, None, :]
        after = col_h[1, r : r + 8, :].astype(F32)[:, None, :]
        spread(1 + r, 8, final_ref[r : r + 8].astype(F32), before, after)
    for side, at, pick in ((0, 0, 7), (1, rows + 1, 0)):
        before = cor_h[2 * side].astype(F32)[pick : pick + 1][:, None, :]
        after = cor_h[2 * side + 1].astype(F32)[pick : pick + 1][:, None, :]
        spread(at, 1, row_h[side].astype(F32)[None], before, after)

    step = 8
    quarter = outs // SHUF
    for r in range(0, rows, step):
        acc = jnp.zeros((step * cols, outs), F32)
        for a in range(3):
            for b in range(3):
                tap = a * 3 + b
                acc = acc + jnp.dot(
                    fb_s[b, r + a : r + a + step].reshape(step * cols, width),
                    wp_s[tap * width : (tap + 1) * width, :],
                    preferred_element_type=F32,
                )
        for k in range(step):
            part = acc[k * cols : (k + 1) * cols]
            slot = k % 2
            for j in range(SHUF):
                pair = j * quarter // 128
                up_s[slot, pl.ds(j, cols, stride=SHUF), :] = part[:, pair * 128 : pair * 128 + 128]
            t = up_s[slot].T
            lanes = lax.broadcasted_iota(jnp.int32, (1, cols * SHUF), 1)
            t = jnp.where(lanes % 2 == 0, t[:quarter], t[quarter : 2 * quarter])
            for c in range(quarter // SHUF):
                image_ref[c, (r + k) * SHUF : (r + k + 1) * SHUF, :] = t[c * SHUF : (c + 1) * SHUF]


def conv_image(sizes, final, left, right, weight):
    rows, cols, width = final.shape
    outs = weight.shape[1]
    vm = pl.BlockSpec(memory_space=pltpu.VMEM)
    return pl.pallas_call(
        functools.partial(conv_kernel, sizes),
        out_shape=jax.ShapeDtypeStruct((outs // SHUF**2, rows * SHUF, cols * SHUF), F32),
        in_specs=[vm] * 4,
        out_specs=vm,
        scratch_shapes=[
            pltpu.VMEM((2, cols, width), BF),
            pltpu.VMEM((2, rows, width), BF),
            pltpu.VMEM((4, 8, width), BF),
            pltpu.VMEM((3, rows + 2, cols, width), BF),
            pltpu.VMEM(weight.shape, BF),
            pltpu.VMEM((2, cols * SHUF, 128), F32),
            pltpu.SemaphoreType.DMA((8,)),
            pltpu.SemaphoreType.DMA((8,)),
        ],
        compiler_params=pltpu.CompilerParams(
            collective_id=1, has_side_effects=True, vmem_limit_bytes=VMEM_LIMIT
        ),
        name="conv_image",
    )(final, left, right, weight)


def local(sizes, field, gains, w_query, w_key, w_value, w_out, w_up, w_down, final_gain, conv_weight):
    rows, cols, width = field.shape
    halo = halo_exchange(sizes, field).reshape(-1, width)
    final, left, right = layer(
        sizes, rows, cols, field.reshape(-1, width), halo, gains[0], w_query[0], w_key[0],
        w_value[0], w_out[0], w_up[0], w_down[0], final_gain[None, :],
    )
    weight = conv_weight.reshape(-1, conv_weight.shape[3])
    return conv_image(sizes, final.reshape(rows, cols, width), left, right, weight)


def solution(mesh):
    sizes = (mesh.shape["row"], mesh.shape["col"])
    return jax.shard_map(
        functools.partial(local, sizes),
        mesh=mesh,
        in_specs=(P("row", "col", None), P(), P(), P(), P(), P(), P(), P(), P(), P()),
        out_specs=P(None, "row", "col"),
        check_vma=False,
    )
```

time: 131 us -> 59.5 us (0.45)
  Pallas kernels: 0 us -> 57.1 us
  matrix products: 47.6 us -> 0 us
  local copies, waits for them, and re-layouts: 30.3 us -> 2.07 us
  starting transfers between devices: 22.9 us -> 0 us
  other arithmetic: 15.9 us -> 0 us
  waiting for transfers between devices: 12.3 us -> 0 us
    pallas_call x0 -> x3, Pallas kernels: none -> 57.1 us  [the longest x1 32.3 us: layer(): pl.pallas_call(functools.partial(layer_kernel, sizes, rows, cols), out_sh...]
    dot_general x31 -> x0, matrix products: 47.6 us -> none  [the longest x8 20.3 us: one_head(): return jnp.dot(weights, v_one, preferred_element_type=jnp.float32)]
    ppermute x8 -> x0, starting transfers between devices: 22.9 us -> none  [the longest x4 16.3 us: extended(): lax.ppermute(lax.slice_in_dim(block, block.shape[dim] - width, None, axis...]
    ppermute x8 -> x0, waiting for transfers between devices: 12.3 us -> none  [the longest x4 12.3 us: extended(): lax.ppermute(lax.slice_in_dim(block, 0, width, axis=dim), axis, backward)]
    reduce_sum x9 -> x0, other arithmetic: 11.4 us -> none  [the longest x8 10.3 us: one_head(): jnp.sum(expo, axis=-1, keepdims=True)]
    another operation x3 -> x0, local copies, waits for them, and re-layouts: 9.97 us -> none  [the longest x1 4.58 us: attend(): k_heads = keys.reshape(width, HEADS, HEAD).transpose(1, 0, 2)]
    reshape x2 -> x0, local copies, waits for them, and re-layouts: 7.93 us -> none  [the longest x1 5.31 us: local(): return image.reshape(OUT_CH, tile_rows * SHUF, tile_cols * SHUF)]
    transpose x1 -> x0, local copies, waits for them, and re-layouts: 6.74 us -> none  [local(): conv.reshape(tile_rows, tile_cols, OUT_CH, SHUF, SHUF)]
  transfers between devices with their start and end apart: 8 -> 0, of which waited for: 4 -> 0; matrix products, arithmetic and copies ran while one was open for 2% -> 0% of each run, Pallas kernels for 0% -> 0%
where the time goes in v1:
time: 59.5 us; the launch traced here: 59.2 us
  Pallas kernels  57.1 us (96%)
  local copies, waits for them, and re-layouts  2.07 us (3%)
    pallas_call x1, Pallas kernels, layer(): pl.pallas_call(functools.partial(layer_kernel, sizes, rows, cols), out_sh...  32.3 us
    pallas_call x1, Pallas kernels, halo_exchange(): pl.pallas_call(functools.partial(halo_kernel, sizes), out_shape=jax.Shape...  13.4 us
    pallas_call x1, Pallas kernels, conv_image(): pl.pallas_call(functools.partial(conv_kernel, sizes), out_shape=jax.Shape...  11.4 us
    unnamed x1, local copies, waits for them, and re-layouts  2.07 us

profile of v1, /device:TPU:1, one launch (start us, length us, event | category | flops | bytes accessed | tf_op | source)
XLA Modules:
  0.0 59.2 jit_solution(6172240531952527485)
XLA Ops:
  0.0 13.4 %halo_exchange.1 = bf16[144,8,256]{2,1,0:T(8,128)(2,1)} custom-call(bf16[24,4,8,256]{3,2,1,0:T(8,128)(2,1)} %bitcast.14), custom_call_target="tpu_custom_call" | custom-call | tf_op jit(solution)/shard_map/halo_exchange/pallas_call | solution.py:116
  13.4 32.3 %layer.1 = (bf16[768,256]{1,0:T(8,128)(2,1)}, bf16[24,256]{1,0:T(8,128)(2,1)}, bf16[24,256]{1,0:T(8,128)(2,1)}) custom-call(bf16[768,256]{1,0:T(8,128)(2,1)} %bitcast.15, bf16[1152,256]{1,0:T(8,128)(2,1)} %bitcast.13, f32[2,256]{1,0:T(2,128)} %bitcast.24, bf16[256,256]{1,0:T(8,128)(2,1)} %bitcast.20, bf16[256,256]{1,0:T(8,128)(2,1)} %bitcast.21, ...), custom_call_target="tpu_custom_call" | custom-call | tf_op jit(solution)/shard_map/layer/pallas_call | solution.py:211
  45.7 11.4 %conv_image.1 = f32[16,96,128]{2,1,0:T(8,128)} custom-call(bf16[24,32,256]{2,1,0:T(8,128)(2,1)} %bitcast.19, bf16[24,256]{1,0:T(8,128)(2,1)} %get-tuple-element.9.left_ref, bf16[24,256]{1,0:T(8,128)(2,1)} %get-tuple-element.10.right_ref, bf16[2304,256]{1,0:T(8,128)(2,1)} %bitcast.16), custom_call_target="tpu_custom_call" | custom-call | tf_op jit(solution)/shard_map/conv_image/pallas_call | solution.py:311
  57.1 2.1 %copy.12 = f32[16,96,128]{2,1,0:T(8,128)} copy(f32[16,96,128]{2,1,0:T(8,128)} %conv_image.1) | data formatting | bytes 1572864

commit v2 on v1

--- a/solution.py
+++ b/solution.py
@@ -10,7 +10,7 @@
 HEADS = 8
 HALO = 8
 SHUF = 4
-CHUNK = 128
+CHUNK = 256
 VMEM_LIMIT = 56 * 1024 * 1024
 BF = jnp.bfloat16
 F32 = jnp.float32
@@ -83,9 +83,8 @@
     return [HALO * groups] * 2 + [rows] * 2 + [HALO] * 4
 
 
-def halo_kernel(sizes, field_ref, halo_ref, send, recv):
+def halo_start(sizes, field_ref, halo_ref, send, recv):
     rows, groups = field_ref.shape[:2]
-    greet(sizes)
     sources, slots, fills = [], [], []
     first = 0
     for step, count in zip(NEIGHBOURS, pieces(rows, groups)):
@@ -94,8 +93,7 @@
         slot = halo_ref.at[pl.ds(first, count)]
         if dc == 0:
             sources.append(field_ref.at[rsel])
-            slot4 = halo_ref.at[pl.ds(first, count)].reshape(HALO, groups, 8, field_ref.shape[3])
-            slots.append(slot4)
+            slots.append(slot.reshape(HALO, groups, 8, field_ref.shape[3]))
         else:
             sources.append(field_ref.at[rsel, 0 if dc < 0 else groups - 1])
             slots.append(slot)
@@ -106,33 +104,30 @@
 
         fills.append(fill)
         first += count
-    finish(swap(sizes, sources, slots, send, recv, fills))
-
-
-def halo_exchange(sizes, field):
-    rows, cols, width = field.shape
-    groups = cols // 8
-    blocks = sum(pieces(rows, groups))
-    return pl.pallas_call(
-        functools.partial(halo_kernel, sizes),
-        out_shape=jax.ShapeDtypeStruct((blocks, 8, width), BF),
-        in_specs=[pl.BlockSpec(memory_space=pltpu.VMEM)],
-        out_specs=pl.BlockSpec(memory_space=pltpu.VMEM),
-        scratch_shapes=[pltpu.SemaphoreType.DMA((8,)), pltpu.SemaphoreType.DMA((8,))],
-        compiler_params=pltpu.CompilerParams(collective_id=0, has_side_effects=True),
-        name="halo_exchange",
-    )(field.reshape(rows, groups, 8, width))
+    return swap(sizes, sources, slots, send, recv, fills)
 
 
 def layer_kernel(
-    sizes, rows, cols,
-    field_ref, halo_ref, gains_ref, wq_ref, wk_ref, wv_ref, wo_ref, wu_ref, wd_ref, fg_ref,
-    out_ref, left_ref, right_ref,
-    q_s, kt_s, va_s, f_s,
+    sizes,
+    field_ref, gains_ref, wq_ref, wk_ref, wv_ref, wo_hbm, wu_hbm, wd_hbm, fg_ref,
+    out_ref, row_h, col_h, cor_h,
+    halo_ref, q_s, kt_s, va_s, f_s, o_s, m_s, left_s, right_s, wo_ref, wu_ref, wd_ref,
+    send, recv, send2, recv2, wsem,
 ):
-    tokens, width = field_ref.shape
+    rows, groups = field_ref.shape[:2]
+    cols = groups * 8
+    tokens, width = q_s.shape
     head = width // HEADS
     per = 128 // head
+    loads = [
+        pltpu.make_async_copy(src, dst, wsem.at[n])
+        for n, (src, dst) in enumerate(((wo_hbm, wo_ref), (wu_hbm, wu_ref), (wd_hbm, wd_ref)))
+    ]
+    for load in loads:
+        load.start()
+    greet(sizes)
+    copies = halo_start(sizes, field_ref, halo_ref, send, recv)
+
     g0 = gains_ref[0:1, :]
     g1 = gains_ref[1:2, :]
     fg = fg_ref[...]
@@ -150,13 +145,36 @@
             va_s[e, start : start + h.shape[0], :] = part.astype(BF)
 
     scale = head**-0.5 * 1.4426950408889634
-    for start in range(0, tokens, 256):
-        h = rms(field_ref[start : start + 256, :].astype(F32), g0).astype(BF)
+    span = CHUNK // cols
+    for start in range(0, tokens, CHUNK):
+        at = start // cols
+        h = rms(field_ref[at : at + span].astype(F32).reshape(CHUNK, width), g0).astype(BF)
         q = jnp.dot(h, wq_ref[...], preferred_element_type=F32) * scale
-        q_s[start : start + 256, :] = q.astype(BF)
+        q_s[start : start + CHUNK, :] = q.astype(BF)
         keep(h, start, None)
+
+    def head_part(at, half, e, first, count):
+        qh = q_s[at, half * 128 : half * 128 + 128]
+        qm = jnp.where(lane == e, qh, jnp.zeros_like(qh))
+        keys = slice(first, first + count)
+        s = jnp.dot(qm, kt_s[half * 128 : half * 128 + 128, keys], preferred_element_type=F32)
+        m = jnp.max(s, axis=-1, keepdims=True)
+        p = jnp.exp2((s - m).astype(BF))
+        return m, jnp.dot(p, va_s[half * per + e, keys, :], preferred_element_type=F32)
+
+    def own(index, carry):
+        at = pl.ds(pl.multiple_of(index * CHUNK, CHUNK), CHUNK)
+        for half in range(width // 128):
+            for e in range(per):
+                m, o = head_part(at, half, e, 0, tokens)
+                o_s[half * per + e, at, :] = o
+                m_s[half * per + e, at, :] = jnp.broadcast_to(m, o.shape)
+        return carry
+
+    lax.fori_loop(0, tokens // CHUNK, own, 0)
+    finish(copies)
+
     first = 0
-    groups = cols // 8
     marks = []
     for step, count in zip(NEIGHBOURS, pieces(rows, groups)):
         ok = there(step, sizes)[0].astype(F32)
@@ -164,35 +182,37 @@
         first += count
     total = first * 8
     for start in range(0, total, 128):
-        h = rms(halo_ref[start : start + 128, :].astype(F32), g0).astype(BF)
+        raw = halo_ref[start // 8 : start // 8 + 16].astype(F32).reshape(128, width)
+        h = rms(raw, g0).astype(BF)
         row = lax.broadcasted_iota(jnp.int32, (128, 1), 0) + start
         ok = jnp.zeros((128, 1), F32)
         for at, count, flag in marks:
             if at < start + 128 and at + count > start:
                 ok = jnp.where((row >= at) & (row < at + count), flag, ok)
         keep(h, tokens + start, ok)
+    for load in loads:
+        load.wait()
 
     def body(index, carry):
         at = pl.ds(pl.multiple_of(index * CHUNK, CHUNK), CHUNK)
         halves = []
         for half in range(width // 128):
-            qh = q_s[at, half * 128 : half * 128 + 128]
             ctx = jnp.zeros((CHUNK, 128), F32)
             for e in range(per):
-                qm = jnp.where(lane == e, qh, jnp.zeros_like(qh))
-                s = jnp.dot(qm, kt_s[half * 128 : half * 128 + 128, :], preferred_element_type=F32)
-                m = jnp.max(s, axis=-1, keepdims=True)
-                p = jnp.exp2(s - m).astype(BF)
-                o = jnp.dot(p, va_s[half * per + e], preferred_element_type=F32)
+                m, o = head_part(at, half, e, tokens, total)
+                old = m_s[half * per + e, at, :]
+                top = jnp.maximum(old, m)
+                o = o * jnp.exp2(m - top) + o_s[half * per + e, at, :] * jnp.exp2(old - top)
                 ctx = jnp.where(lane == e, o / pltpu.roll(o, head, 1), ctx)
             halves.append(ctx.astype(BF))
         ctx = jnp.concatenate(halves, axis=1)
-        x = field_ref[at, :].astype(F32) + jnp.dot(ctx, wo_ref[...], preferred_element_type=F32)
+        x = field_ref[pl.ds(index * span, span)].astype(F32).reshape(CHUNK, width)
+        x = x + jnp.dot(ctx, wo_ref[...], preferred_element_type=F32)
         h = rms(x, g1).astype(BF)
         u = jax.nn.gelu(jnp.dot(h, wu_ref[...], preferred_element_type=F32)).astype(BF)
         x = x + jnp.dot(u, wd_ref[...], preferred_element_type=F32)
         f = rms(x, fg)
-        out_ref[at, :] = f.astype(BF)
+        out_ref[pl.ds(index * span, span)] = f.reshape(span, cols, width).astype(BF)
         for half in range(width // 128):
             f_s[half, at, :] = f[:, half * 128 : half * 128 + 128]
         return carry
@@ -200,57 +220,69 @@
     lax.fori_loop(0, tokens // CHUNK, body, 0)
     for half in range(width // 128):
         sl = slice(half * 128, half * 128 + 128)
-        left_ref[:, sl] = f_s[half, pl.ds(0, rows, stride=cols), :].astype(BF)
-        right_ref[:, sl] = f_s[half, pl.ds(cols - 1, rows, stride=cols), :].astype(BF)
-
-
-def layer(sizes, rows, cols, field, halo, gains, wq, wk, wv, wo, wu, wd, fg):
-    tokens, width = field.shape
-    keys = tokens + halo.shape[0]
+        left_s[:, sl] = f_s[half, pl.ds(0, rows, stride=cols), :].astype(BF)
+        right_s[:, sl] = f_s[half, pl.ds(cols - 1, rows, stride=cols), :].astype(BF)
+    slots = [row_h.at[0], row_h.at[1], col_h.at[0], col_h.at[1]] + [cor_h.at[n] for n in range(4)]
+    sources = [
+        out_ref.at[0], out_ref.at[rows - 1], left_s, right_s,
+        left_s.at[pl.ds(0, 8)], right_s.at[pl.ds(0, 8)],
+        left_s.at[pl.ds(rows - 8, 8)], right_s.at[pl.ds(rows - 8, 8)],
+    ]
+
+    def filler(slot):
+        def fill():
+            slot[...] = jnp.zeros(slot.shape, BF)
+        return fill
+
+    finish(swap(sizes, sources, slots, send2, recv2, [filler(s) for s in slots]))
+
+
+def layer(sizes, field, gains, wq, wk, wv, wo, wu, wd, fg):
+    rows, cols, width = field.shape
+    groups = cols // 8
+    tokens = rows * cols
+    blocks = sum(pieces(rows, groups))
+    keys = tokens + blocks * 8
     vm = pl.BlockSpec(memory_space=pltpu.VMEM)
+    hbm = pl.BlockSpec(memory_space=pl.ANY)
+    eight = pltpu.SemaphoreType.DMA((8,))
     return pl.pallas_call(
-        functools.partial(layer_kernel, sizes, rows, cols),
+        functools.partial(layer_kernel, sizes),
         out_shape=(
-            jax.ShapeDtypeStruct((tokens, width), BF),
-            jax.ShapeDtypeStruct((rows, width), BF),
-            jax.ShapeDtypeStruct((rows, width), BF),
+            jax.ShapeDtypeStruct((rows, cols, width), BF),
+            jax.ShapeDtypeStruct((2, cols, width), BF),
+            jax.ShapeDtypeStruct((2, rows, width), BF),
+            jax.ShapeDtypeStruct((4, 8, width), BF),
         ),
-        in_specs=[vm] * 10,
-        out_specs=(vm, vm, vm),
+        in_specs=[vm] * 5 + [hbm] * 3 + [vm],
+        out_specs=(vm,) * 4,
         scratch_shapes=[
+            pltpu.VMEM((blocks, 8, width), BF),
             pltpu.VMEM((tokens, width), BF),
             pltpu.VMEM((width, keys), BF),
             pltpu.VMEM((HEADS, keys, 128), BF),
             pltpu.VMEM((width // 128, tokens, 128), F32),
+            pltpu.VMEM((HEADS, tokens, 128), F32),
+            pltpu.VMEM((HEADS, tokens, 128), F32),
+            pltpu.VMEM((rows, width), BF),
+            pltpu.VMEM((rows, width), BF),
+            pltpu.VMEM(wo.shape, BF),
+            pltpu.VMEM(wu.shape, BF),
+            pltpu.VMEM(wd.shape, BF),
+            eight, eight, eight, eight,
+            pltpu.SemaphoreType.DMA((3,)),
         ],
-        compiler_params=pltpu.CompilerParams(vmem_limit_bytes=VMEM_LIMIT),
+        compiler_params=pltpu.CompilerParams(
+            collective_id=0, has_side_effects=True, vmem_limit_bytes=VMEM_LIMIT
+        ),
         name="layer",
-    )(field, halo, gains, wq, wk, wv, wo, wu, wd, fg)
-
-
-def conv_kernel(
-    sizes,
-    final_ref, left_ref, right_ref, weight_ref,
-    image_ref,
-    row_h, col_h, cor_h, fb_s, wp_s, up_s, send, recv,
-):
+    )(field.reshape(rows, groups, 8, width), gains, wq, wk, wv, wo, wu, wd, fg)
+
+
+def conv_kernel(final_ref, row_h, col_h, cor_h, weight_ref, image_ref, fb_s, wp_s, up_s):
     rows, cols, width = final_ref.shape
     tokens = rows * cols
     outs = weight_ref.shape[1]
-    greet(sizes)
-    slots = [row_h.at[0], row_h.at[1], col_h.at[0], col_h.at[1]] + [cor_h.at[n] for n in range(4)]
-    sources = [
-        final_ref.at[0], final_ref.at[rows - 1], left_ref, right_ref,
-        left_ref.at[pl.ds(0, 8)], right_ref.at[pl.ds(0, 8)],
-        left_ref.at[pl.ds(rows - 8, 8)], right_ref.at[pl.ds(rows - 8, 8)],
-    ]
-
-    def filler(slot):
-        def fill():
-            slot[...] = jnp.zeros(slot.shape, BF)
-        return fill
-
-    copies = swap(sizes, sources, slots, send, recv, [filler(s) for s in slots])
     old = lax.broadcasted_iota(jnp.int32, (outs, outs), 0)
     new = lax.broadcasted_iota(jnp.int32, (outs, outs), 1)
     want = (new % (outs // SHUF)) * SHUF + new // (outs // SHUF)
@@ -258,8 +290,6 @@
     for tap in range(9):
         sl = slice(tap * width, (tap + 1) * width)
         wp_s[sl, :] = jnp.dot(weight_ref[sl, :], perm, preferred_element_type=F32).astype(BF)
-    finish(copies)
-
     col = lax.broadcasted_iota(jnp.int32, (1, cols, 1), 1)
 
     def spread(first, count, x, before, after):
@@ -304,41 +334,32 @@
                 image_ref[c, (r + k) * SHUF : (r + k + 1) * SHUF, :] = t[c * SHUF : (c + 1) * SHUF]
 
 
-def conv_image(sizes, final, left, right, weight):
+def conv_image(final, row, col, corner, weight):
     rows, cols, width = final.shape
     outs = weight.shape[1]
     vm = pl.BlockSpec(memory_space=pltpu.VMEM)
     return pl.pallas_call(
-        functools.partial(conv_kernel, sizes),
+        conv_kernel,
         out_shape=jax.ShapeDtypeStruct((outs // SHUF**2, rows * SHUF, cols * SHUF), F32),
-        in_specs=[vm] * 4,
+        in_specs=[vm] * 5,
         out_specs=vm,
         scratch_shapes=[
-            pltpu.VMEM((2, cols, width), BF),
-            pltpu.VMEM((2, rows, width), BF),
-            pltpu.VMEM((4, 8, width), BF),
             pltpu.VMEM((3, rows + 2, cols, width), BF),
             pltpu.VMEM(weight.shape, BF),
             pltpu.VMEM((2, cols * SHUF, 128), F32),
-            pltpu.SemaphoreType.DMA((8,)),
-            pltpu.SemaphoreType.DMA((8,)),
         ],
-        compiler_params=pltpu.CompilerParams(
-            collective_id=1, has_side_effects=True, vmem_limit_bytes=VMEM_LIMIT
-        ),
+        compiler_params=pltpu.CompilerParams(vmem_limit_bytes=VMEM_LIMIT),
         name="conv_image",
-    )(final, left, right, weight)
+    )(final, row, col, corner, weight)
 
 
 def local(sizes, field, gains, w_query, w_key, w_value, w_out, w_up, w_down, final_gain, conv_weight):
-    rows, cols, width = field.shape
-    halo = halo_exchange(sizes, field).reshape(-1, width)
-    final, left, right = layer(
-        sizes, rows, cols, field.reshape(-1, width), halo, gains[0], w_query[0], w_key[0],
-        w_value[0], w_out[0], w_up[0], w_down[0], final_gain[None, :],
+    final, row, col, corner = layer(
+        sizes, field, gains[0], w_query[0], w_key[0], w_value[0], w_out[0], w_up[0], w_down[0],
+        final_gain[None, :],
     )
     weight = conv_weight.reshape(-1, conv_weight.shape[3])
-    return conv_image(sizes, final.reshape(rows, cols, width), left, right, weight)
+    return conv_image(final, row, col, corner, weight)
 
 
 def solution(mesh):

time: 59.5 us -> 41.2 us (0.69)
  Pallas kernels: 57.1 us -> 40.9 us
  local copies, waits for them, and re-layouts: 2.07 us -> 0 us
    pallas_call x3 -> x2, Pallas kernels: 57.1 us -> 40.9 us  [the longest x1 36.8 us: layer(): pl.pallas_call(functools.partial(layer_kernel, sizes), out_shape=(jax.Sha...]
    unnamed x1 -> x0, local copies, waits for them, and re-layouts: 2.07 us -> none
where the time goes in v2:
time: 41.2 us; the launch traced here: 40.9 us
  Pallas kernels  40.9 us (99%)
    pallas_call x1, Pallas kernels, layer(): pl.pallas_call(functools.partial(layer_kernel, sizes), out_shape=(jax.Sha...  36.8 us
    pallas_call x1, Pallas kernels, conv_image(): pl.pallas_call(conv_kernel, out_shape=jax.ShapeDtypeStruct((outs // SHUF...  4.14 us

profile of v2, /device:TPU:1, one launch (start us, length us, event | category | flops | bytes accessed | tf_op | source)
XLA Modules:
  0.0 40.9 jit_solution(11866528791742913132)
XLA Ops:
  0.0 36.8 %layer.1 = (bf16[24,32,256]{2,1,0:T(8,128)(2,1)}, bf16[2,32,256]{2,1,0:T(8,128)(2,1)}, bf16[2,24,256]{2,1,0:T(8,128)(2,1)}, bf16[4,8,256]{2,1,0:T(8,128)(2,1)}) custom-call(bf16[24,4,8,256]{3,2,1,0:T(8,128)(2,1)} %bitcast.13, f32[2,256]{1,0:T(2,128)} %bitcast.18, bf16[256,256]{1,0:T(8,128)(2,1)} %bitcast.14, bf16[256,256]{1,0:T(8,128)(2,1)} %bitcast.15, ...), custom_call_target="tpu_custom_call" | custom-call | tf_op jit(solution)/shard_map/layer/pallas_call | solution.py:249
  36.8 4.1 %conv_image.1 = f32[16,96,128]{2,1,0:T(8,128)} custom-call(bf16[24,32,256]{2,1,0:T(8,128)(2,1)} %get-tuple-element.9.final_ref, bf16[2,32,256]{2,1,0:T(8,128)(2,1)} %get-tuple-element.10.row_h, bf16[2,24,256]{2,1,0:T(8,128)(2,1)} %get-tuple-element.11.col_h, bf16[4,8,256]{2,1,0:T(8,128)(2,1)} %get-tuple-element.12.cor_h, bf16[2304,256]{1,0:T(8,128)(2,1)} %bitcast.10), custom_call_target="tpu_custom_call" | custom-call | tf_op jit(solution)/shard_map/conv_image/pallas_call | solution.py:341
